TPU v7x, 512 devices: a whole 4x8x8 slice. The times are simulated.
512 devices in a mesh: list: 32 (over y_hi, x, core), shard: 16 (over z, y_lo).
Axes of the slice: x: 4, y: 8 (y_hi: 4, y_lo: 2; y = y_hi * 2 + y_lo), z: 8, core: 2. Of those that a mesh axis runs over, the one named last changes fastest.
Arguments:
- features: bfloat16 [4096, 4096], P(('list', 'shard')), may hold values from -6 to 6
- norm_gain: float32 [4096], replicated, may hold values from 0.5 to 1.5
- gate_weight: bfloat16 [4096, 11008], P('shard', 'list'), may hold values from -0.09375 to 0.09375
- up_weight: bfloat16 [4096, 11008], P('shard', 'list'), may hold values from -0.09375 to 0.09375
- down_weight: bfloat16 [11008, 4096], P('list', 'shard'), may hold values from -0.0546875 to 0.0546875
- centroids: float32 [64, 4096], P('list'), may hold values from -6 to 6
- list_ids: int32 [4096], P(('list', 'shard')), may hold values from 0 to 63
- live: int32 [4096], P(('list', 'shard')), may hold values 0 or 1
Outputs:
- residuals: bfloat16 [4096, 4096], P(('list', 'shard'))
- refreshed: float32 [64, 4096], P('list')
All inputs are finite; a program needn't handle non-finite values. No bound on the sum of `live` on one device may be relied on, other than what follows from the above.
Results may differ from a plain program's by a relative error of at most 0.015.
Values may be sent and summed in bfloat16 or wider, within the bound.
No kernel may reach another device: no remote copies, remote signals or barrier semaphores. Data moves between devices by JAX's collectives and lax.ppermute only.
A program may use at most 64 MiB of HBM per device.

v0:
```python
import jax
import jax.numpy as jnp
from jax import lax
from jax.sharding import PartitionSpec as P


def laid_out(parts, dim):
    shape = list(parts.shape[1:])
    shape[dim] *= parts.shape[0]
    return jnp.moveaxis(parts, 0, dim).reshape(shape)


def from_everyone(value, axis):
    copies = jnp.broadcast_to(value, (lax.axis_size(axis), *value.shape))
    return lax.all_to_all(copies, axis, split_axis=0, concat_axis=0, tiled=True)


def collect(value, axis, dim):
    return laid_out(from_everyone(value, axis), dim)


def in_one_piece(arrays, axis, dim, along):
    both = jnp.concatenate(arrays, axis=along)
    filled, at, done = (lax.all_gather(both, axis, axis=dim, tiled=True), 0, [])
    for a in arrays:
        done.append(lax.slice_in_dim(filled, at, at + a.shape[along], axis=along))
        at += a.shape[along]
    return tuple(done)


def split_up(value, dim, peers):
    before, after = (value.shape[:dim], value.shape[dim + 1 :])
    return jnp.moveaxis(value.reshape(*before, peers, -1, *after), dim, 0)


def sum_at_owner(value, axis, dim):
    peers = lax.axis_size(axis)
    parts = lax.all_to_all(split_up(value, dim, peers), axis, 0, 0, tiled=True)
    return jnp.sum(parts.astype(jnp.float32), axis=0)


def sent_together(arrays, axis, dim, along):
    columns = [a.reshape(*a.shape[:along], -1) for a in arrays]
    both = jnp.concatenate(columns, axis=along)
    filled, at, done = (sum_at_owner(both, axis, dim), 0, [])
    for a, column in zip(arrays, columns):
        share = filled[..., at : at + column.shape[along]]
        done.append(share.reshape(*share.shape[:along], *a.shape[along:]))
        at += column.shape[along]
    return tuple(done)


def taken_together(value, axis):
    return from_everyone(value, axis).astype(jnp.float32).sum(axis=0)


def body(features, norm_gain, gate_weight, up_weight, down_weight, centroids, list_ids, live):
    group_rows = collect(features, "list", 0)
    pieces = in_one_piece((gate_weight, up_weight), "shard", 0, 1)
    first = jnp.dot(group_rows, pieces[0], preferred_element_type=jnp.float32)
    second = jnp.dot(group_rows, pieces[1], preferred_element_type=jnp.float32)
    hidden = (jax.nn.silu(first) * second).astype(jnp.bfloat16)
    partial_sums = jnp.dot(
        hidden,
        lax.all_gather(down_weight, "shard", axis=1, tiled=True),
        preferred_element_type=jnp.float32,
    )
    mixed = sum_at_owner(partial_sums.astype(jnp.bfloat16), "list", 0)
    stream = features.astype(jnp.float32) + mixed
    scale = lax.rsqrt(jnp.mean(stream * stream, axis=1, keepdims=True) + 1e-05)
    embedding = (stream * scale * norm_gain).astype(jnp.bfloat16)
    table = lax.all_gather(centroids.astype(jnp.bfloat16), "list", axis=0, tiled=True)
    list_total = table.shape[0]
    alive = live.astype(jnp.float32)
    member = (list_ids[:, None] == jnp.arange(list_total, dtype=jnp.int32)[None, :]).astype(
        jnp.float32
    )
    picked = jnp.dot(member.astype(jnp.bfloat16), table, preferred_element_type=jnp.float32)
    residuals = (alive[:, None] * (embedding.astype(jnp.float32) - picked)).astype(jnp.bfloat16)
    weighted = member * alive[:, None]
    dense_sums = jnp.dot(weighted.T, embedding.astype(jnp.float32), precision=lax.Precision.HIGHEST)
    dense_counts = jnp.sum(weighted, axis=0)
    owned_sums, owned_counts = sent_together(
        (dense_sums.astype(jnp.bfloat16), dense_counts.astype(jnp.bfloat16)), "list", 0, 1
    )
    total_sums, total_counts = (
        taken_together(owned_sums.astype(jnp.bfloat16), "shard").astype(jnp.float32),
        taken_together(owned_counts.astype(jnp.bfloat16), "shard").astype(jnp.float32),
    )
    refreshed = (centroids + total_sums) / (1.0 + total_counts[:, None])
    return (residuals, refreshed)


def solution(mesh):
    in_specs = (
        P(("list", "shard"), None),
        P(),
        P("shard", "list"),
        P("shard", "list"),
        P("list", "shard"),
        P("list", None),
        P(("list", "shard")),
        P(("list", "shard")),
    )
    out_specs = (P(("list", "shard"), None), P("list", None))
    return jax.shard_map(body, mesh=mesh, in_specs=in_specs, out_specs=out_specs, check_vma=False)
```

profile of v0, /device:TPU:1, one launch (start us, length us, event | category | flops | bytes accessed | tf_op | source)
XLA Modules:
  0.0 452.9 jit_solution(17762954597065309443)
XLA Ops:
  7.2 1.8 pad_maximum_fusion.1
  9.1 0.7 all-gather.6.cloned.1.call-update
  9.8 1.1 broadcast_in_dim.6
  10.9 81.3 %all_to_all.26 = bf16[32,8,4096]{2,1,0:T(8,128)(2,1)S(1)} all-to-all(bf16[32,8,4096]{2,1,0:T(8,128)(2,1)S(1)} %broadcast_in_dim.6), channel_id=1, replica_groups=mesh['list'=32,'shard'=16] {'list'}, dimensions={0} | all-to-all | bytes 4194304 | tf_op jit(solution)/shard_map/all_to_all | solution.py:15
  92.2 94.7 %all-gather.4.cloned.1.call-done = bf16[4096,688]{0,1:T(8,128)(2,1)} async-done(((bf16[256,688]{0,1:T(8,128)(2,1)}), bf16[4096,688]{0,1:T(8,128)(2,1)}) %all-gather.4.cloned.1.call-update) | async-done | bytes 5636112 | tf_op jit(solution)/shard_map/all_gather | solution.py:24
  186.9 2.9 fusion.9
  189.8 77.1 %all-gather.6.cloned.1.call-done = bf16[344,4096]{1,0:T(8,128)(2,1)} async-done(((bf16[344,256]{1,0:T(8,128)(2,1)}), bf16[344,4096]{1,0:T(8,128)(2,1)}) %all-gather.6.cloned.1.call-update) | async-done | bytes 2818064 | tf_op jit(solution)/shard_map/all_gather | solution.py:65
  266.9 7.7 %fusion = bf16[32,8,4096]{2,1,0:T(8,128)(2,1)} fusion(bf16[344,4096]{1,0:T(8,128)(2,1)} %all-gather.6.cloned.1.call-done, bf16[32,8,4096]{2,1,0:T(8,128)(2,1)S(1)} %all_to_all.26, bf16[4096,688]{0,1:T(8,128)(2,1)} %all-gather.4.cloned.1.call-done, f32[256,344]{0,1:T(8,128)S(1)} %fusion.9), kind=kOutput, calls=%fused_computation.1 | convolution fusion | flops 1444417536 | bytes 10182656 | tf_op jit(solution)/shard_map/dot_general | solution.py:63
  274.6 19.3 %all-to-all-start.1 = ((bf16[32,8,4096]{2,1,0:T(8,128)(2,1)}), bf16[32,8,4096]{2,1,0:T(8,128)(2,1)S(1)}, u32[]{:S(2)}, u32[]{:S(2)}) async-start(bf16[32,8,4096]{2,1,0:T(8,128)(2,1)} %fusion), calls=%async_computation.1 | async-start | bytes 4194304 | tf_op jit(solution)/shard_map/all_to_all | solution.py:38
  294.1 0.1 convert_element_type.84
  294.2 50.7 %all-to-all-done.1 = bf16[32,8,4096]{2,1,0:T(8,128)(2,1)S(1)} async-done(((bf16[32,8,4096]{2,1,0:T(8,128)(2,1)}), bf16[32,8,4096]{2,1,0:T(8,128)(2,1)S(1)}, u32[]{:S(2)}, u32[]{:S(2)}) %all-to-all-start.1) | async-done | bytes 2097184 | tf_op jit(solution)/shard_map/all_to_all | solution.py:38
  344.9 0.3 convert_reduce_fusion
  345.2 0.2 multiply_reduce_fusion
  345.5 0.7 convolution_convert_fusion.1
  346.2 0.3 concatenate.10
  346.5 0.5 pad_maximum_fusion
  347.1 23.8 %all_to_all.27 = bf16[32,2,4097]{2,1,0:T(2,128)(2,1)S(1)} all-to-all(bf16[32,2,4097]{2,1,0:T(2,128)(2,1)S(1)} %pad_maximum_fusion), channel_id=1, replica_groups=mesh['list'=32,'shard'=16] {'list'}, dimensions={0} | all-to-all | bytes 1048832 | tf_op jit(solution)/shard_map/all_to_all | solution.py:38
  370.9 0.4 reduce.1
  371.4 0.1 slice_reduce_fusion
  371.5 0.6 broadcast_in_dim.8
  372.1 5.5 %all-to-all-start.4 = ((bf16[16,1,2]{2,1,0:T(2,128)(2,1)}), bf16[16,1,2]{2,1,0:T(2,128)(2,1)S(1)}, u32[]{:S(2)}, u32[]{:S(2)}) async-start(bf16[16,1,2]{2,1,0:T(2,128)(2,1)} %broadcast_in_dim.8), calls=%async_computation.4 | async-start | bytes 16384 | tf_op jit(solution)/shard_map/all_to_all | solution.py:15
  377.6 7.3 %all-to-all-done.4 = bf16[16,1,2]{2,1,0:T(2,128)(2,1)S(1)} async-done(((bf16[16,1,2]{2,1,0:T(2,128)(2,1)}), bf16[16,1,2]{2,1,0:T(2,128)(2,1)S(1)}, u32[]{:S(2)}, u32[]{:S(2)}) %all-to-all-start.4) | async-done | bytes 96 | tf_op jit(solution)/shard_map/all_to_all | solution.py:15
  384.9 0.9 broadcast_in_dim.7
  385.8 3.5 all-to-all-start.3
  389.3 0.1 copy.21
  389.4 0.1 convert_reduce_fusion.2
  389.5 8.6 %all-to-all-done.3 = bf16[16,2,4096]{2,1,0:T(2,128)(2,1)S(1)} async-done(((bf16[16,2,4096]{2,1,0:T(2,128)(2,1)}), bf16[16,2,4096]{2,1,0:T(2,128)(2,1)S(1)}, u32[]{:S(2)}, u32[]{:S(2)}) %all-to-all-start.3) | async-done | bytes 262176 | tf_op jit(solution)/shard_map/all_to_all | solution.py:15
  398.1 0.2 convert_reduce_fusion.1
  398.4 0.7 add_divide_fusion
  399.1 46.0 %all-gather = bf16[32,2,4096]{2,1,0:T(2,128)(2,1)S(1)} all-gather(bf16[1,2,4096]{2,1,0:T(2,128)(2,1)S(1)} %get-tuple-element.3), channel_id=1, replica_groups=mesh['list'=32,'shard'=16] {'list'}, dimensions={0}, use_global_device_ids=true | all-gather | bytes 540672 | tf_op jit(solution)/shard_map/all_gather | solution.py:72
  445.0 0.2 reshape.51
  445.2 0.9 fusion.2
  (19 shorter events, 0.3 us)
Async XLA Ops:
  7.2 179.7 %all-gather.4.cloned.1.call-start = ((), (), s32[]{:S(2)}) async-start(), calls=%async_computation.5 | async-start | bytes 5988352 | tf_op jit(solution)/shard_map/all_gather | solution.py:24
  9.0 257.9 %all-gather.6.cloned.1.call-start = ((), (), s32[]{:S(2)}) async-start(), calls=%async_computation.6 | async-start | bytes 2994176 | tf_op jit(solution)/shard_map/all_gather | solution.py:65
  274.6 19.3 %copy-start.4 = (s32[8]{0:T(128)S(1)}, s32[8]{0:T(128)}, u32[]{:S(2)}) copy-start(s32[8]{0:T(128)} %param.15) | copy-start | bytes 100
  274.6 19.4 %copy-start.3 = (s32[8]{0:T(128)S(1)}, s32[8]{0:T(128)}, u32[]{:S(2)}) copy-start(s32[8]{0:T(128)} %param.14) | copy-start | bytes 100
  274.6 70.6 %copy-start = (bf16[8,4096]{1,0:T(8,128)(2,1)S(1)}, bf16[8,4096]{1,0:T(8,128)(2,1)}, u32[]{:S(2)}) copy-start(bf16[8,4096]{1,0:T(8,128)(2,1)} %param.8) | copy-start | bytes 196612
  274.6 70.8 %copy-start.2 = (f32[4096]{0:T(1024)S(1)}, f32[4096]{0:T(1024)}, u32[]{:S(2)}) copy-start(f32[4096]{0:T(1024)} %param.9) | copy-start | bytes 49156
  274.6 70.3 %all-to-all-start.1 = ((bf16[32,8,4096]{2,1,0:T(8,128)(2,1)}), bf16[32,8,4096]{2,1,0:T(8,128)(2,1)S(1)}, u32[]{:S(2)}, u32[]{:S(2)}) async-start(bf16[32,8,4096]{2,1,0:T(8,128)(2,1)} %fusion), calls=%async_computation.1 | async-start | bytes 4194304 | tf_op jit(solution)/shard_map/all_to_all | solution.py:38
  345.5 52.9 %copy-start.1 = (f32[2,4096]{1,0:T(2,128)S(1)}, f32[2,4096]{1,0:T(2,128)}, u32[]{:S(2)}) copy-start(f32[2,4096]{1,0:T(2,128)} %param.13) | copy-start | bytes 98308
  372.1 12.8 %all-to-all-start.4 = ((bf16[16,1,2]{2,1,0:T(2,128)(2,1)}), bf16[16,1,2]{2,1,0:T(2,128)(2,1)S(1)}, u32[]{:S(2)}, u32[]{:S(2)}) async-start(bf16[16,1,2]{2,1,0:T(2,128)(2,1)} %broadcast_in_dim.8), calls=%async_computation.4 | async-start | bytes 16384 | tf_op jit(solution)/shard_map/all_to_all | solution.py:15
  385.8 12.4 %all-to-all-start.3 = ((bf16[16,2,4096]{2,1,0:T(2,128)(2,1)}), bf16[16,2,4096]{2,1,0:T(2,128)(2,1)S(1)}, u32[]{:S(2)}, u32[]{:S(2)}) async-start(bf16[16,2,4096]{2,1,0:T(2,128)(2,1)} %broadcast_in_dim.7), calls=%async_computation.3 | async-start | bytes 524288 | tf_op jit(solution)/shard_map/all_to_all | solution.py:15
Sparse Core Ops, SparseCore 0:
  10.0 176.8 all-gather.3
  188.9 77.9 all-gather.5
where the time goes:
time: 453 us
  waiting for transfers between devices  239 us (53%)
  blocking collectives  151 us (33%)
  starting transfers between devices  28.4 us (6%)
  between operations  14.2 us (3%)
  matrix products  12.2 us (3%)
    all_gather x1, waiting for transfers between devices, in_one_piece(): filled, at, done = (lax.all_gather(both, axis, axis=dim, tiled=True), 0, [])  94.7 us
    all_to_all x1, blocking collectives, from_everyone(): return lax.all_to_all(copies, axis, split_axis=0, concat_axis=0, tiled=True)  81.3 us
    all_gather x1, waiting for transfers between devices, body(): lax.all_gather(down_weight, 'shard', axis=1, tiled=True)  77.1 us
    all_to_all x1, waiting for transfers between devices, sum_at_owner(): parts = lax.all_to_all(split_up(value, dim, peers), axis, 0, 0, tiled=True)  50.7 us
    all_gather x1, blocking collectives, body(): lax.all_gather(centroids.astype(jnp.bfloat16), 'list', axis=0, tiled=True)  46 us
    all_to_all x1, blocking collectives, sum_at_owner(): parts = lax.all_to_all(split_up(value, dim, peers), axis, 0, 0, tiled=True)  23.8 us
    all_to_all x1, starting transfers between devices, sum_at_owner(): parts = lax.all_to_all(split_up(value, dim, peers), axis, 0, 0, tiled=True)  19.3 us
    all_to_all x2, waiting for transfers between devices, from_everyone(): return lax.all_to_all(copies, axis, split_axis=0, concat_axis=0, tiled=True)  15.9 us
  transfers between devices with their start and end apart: 5, of which 5 were waited for; matrix products, arithmetic and copies ran while one was open for 1% of the time, Pallas kernels for 0%

commit v1 on v0

--- a/solution.py
+++ b/solution.py
@@ -69,7 +69,12 @@
     stream = features.astype(jnp.float32) + mixed
     scale = lax.rsqrt(jnp.mean(stream * stream, axis=1, keepdims=True) + 1e-05)
     embedding = (stream * scale * norm_gain).astype(jnp.bfloat16)
-    table = lax.all_gather(centroids.astype(jnp.bfloat16), "list", axis=0, tiled=True)
+    table = jnp.concatenate(
+        lax.all_to_all(
+            jnp.stack([centroids.astype(jnp.bfloat16)] * lax.axis_size("list")), "list", 0, 0
+        ),
+        axis=0,
+    )
     list_total = table.shape[0]
     alive = live.astype(jnp.float32)
     member = (list_ids[:, None] == jnp.arange(list_total, dtype=jnp.int32)[None, :]).astype(

time: 453 us -> 432 us (0.954)
  blocking collectives: 151 us -> 129 us
    all_gather x1 -> x0, blocking collectives: 46 us -> none  [body(): lax.all_gather(centroids.astype(jnp.bfloat16), 'list', axis=0, tiled=True)]
    all_to_all x0 -> x1, blocking collectives: none -> 24 us  [body(): lax.all_to_all(jnp.stack([centroids.astype(jnp.bfloat16)] * lax.axis_size...]
where the time goes in v1:
time: 432 us; the launch traced here: 431 us
  waiting for transfers between devices  239 us (55%)
  blocking collectives  129 us (30%)
  starting transfers between devices  28.4 us (7%)
  between operations  14.2 us (3%)
  matrix products  12.2 us (3%)
  other arithmetic  4.44 us (1%)
    all_gather x1, waiting for transfers between devices, in_one_piece(): filled, at, done = (lax.all_gather(both, axis, axis=dim, tiled=True), 0, [])  94.7 us
    all_to_all x1, blocking collectives, from_everyone(): return lax.all_to_all(copies, axis, split_axis=0, concat_axis=0, tiled=True)  81.3 us
    all_gather x1, waiting for transfers between devices, body(): lax.all_gather(down_weight, 'shard', axis=1, tiled=True)  77.1 us
    all_to_all x1, waiting for transfers between devices, sum_at_owner(): parts = lax.all_to_all(split_up(value, dim, peers), axis, 0, 0, tiled=True)  50.7 us
    all_to_all x1, blocking collectives, body(): lax.all_to_all(jnp.stack([centroids.astype(jnp.bfloat16)] * lax.axis_size...  24 us
    all_to_all x1, blocking collectives, sum_at_owner(): parts = lax.all_to_all(split_up(value, dim, peers), axis, 0, 0, tiled=True)  23.8 us
    all_to_all x1, starting transfers between devices, sum_at_owner(): parts = lax.all_to_all(split_up(value, dim, peers), axis, 0, 0, tiled=True)  19.3 us
    all_to_all x2, waiting for transfers between devices, from_everyone(): return lax.all_to_all(copies, axis, split_axis=0, concat_axis=0, tiled=True)  15.9 us
  transfers between devices with their start and end apart: 5, of which 5 were waited for; matrix products, arithmetic and copies ran while one was open for 1% of the time, Pallas kernels for 0%

profile of v1, /device:TPU:1, one launch (start us, length us, event | category | flops | bytes accessed | tf_op | source)
XLA Modules:
  0.0 431.5 jit_solution(15466986259958730046)
XLA Ops:
  7.2 1.8 pad_maximum_fusion.1
  9.1 0.7 all-gather.5.cloned.1.call-update
  9.8 1.1 broadcast_in_dim.6
  10.9 81.3 %all_to_all.31 = bf16[32,8,4096]{2,1,0:T(8,128)(2,1)S(1)} all-to-all(bf16[32,8,4096]{2,1,0:T(8,128)(2,1)S(1)} %broadcast_in_dim.6), channel_id=1, replica_groups=mesh['list'=32,'shard'=16] {'list'}, dimensions={0} | all-to-all | bytes 4194304 | tf_op jit(solution)/shard_map/all_to_all | solution.py:15
  92.2 94.7 %all-gather.3.cloned.1.call-done = bf16[4096,688]{0,1:T(8,128)(2,1)} async-done(((bf16[256,688]{0,1:T(8,128)(2,1)}), bf16[4096,688]{0,1:T(8,128)(2,1)}) %all-gather.3.cloned.1.call-update) | async-done | bytes 5636112 | tf_op jit(solution)/shard_map/all_gather | solution.py:24
  186.9 2.9 fusion.9
  189.8 77.1 %all-gather.5.cloned.1.call-done = bf16[344,4096]{1,0:T(8,128)(2,1)} async-done(((bf16[344,256]{1,0:T(8,128)(2,1)}), bf16[344,4096]{1,0:T(8,128)(2,1)}) %all-gather.5.cloned.1.call-update) | async-done | bytes 2818064 | tf_op jit(solution)/shard_map/all_gather | solution.py:65
  266.9 7.7 %fusion = bf16[32,8,4096]{2,1,0:T(8,128)(2,1)} fusion(bf16[344,4096]{1,0:T(8,128)(2,1)} %all-gather.5.cloned.1.call-done, bf16[32,8,4096]{2,1,0:T(8,128)(2,1)S(1)} %all_to_all.31, bf16[4096,688]{0,1:T(8,128)(2,1)} %all-gather.3.cloned.1.call-done, f32[256,344]{0,1:T(8,128)S(1)} %fusion.9), kind=kOutput, calls=%fused_computation.1 | convolution fusion | flops 1444417536 | bytes 10182656 | tf_op jit(solution)/shard_map/dot_general | solution.py:63
  274.6 19.3 %all-to-all-start.1 = ((bf16[32,8,4096]{2,1,0:T(8,128)(2,1)}), bf16[32,8,4096]{2,1,0:T(8,128)(2,1)S(1)}, u32[]{:S(2)}, u32[]{:S(2)}) async-start(bf16[32,8,4096]{2,1,0:T(8,128)(2,1)} %fusion), calls=%async_computation.1 | async-start | bytes 4194304 | tf_op jit(solution)/shard_map/all_to_all | solution.py:38
  294.1 0.1 convert_element_type.84
  294.2 50.7 %all-to-all-done.1 = bf16[32,8,4096]{2,1,0:T(8,128)(2,1)S(1)} async-done(((bf16[32,8,4096]{2,1,0:T(8,128)(2,1)}), bf16[32,8,4096]{2,1,0:T(8,128)(2,1)S(1)}, u32[]{:S(2)}, u32[]{:S(2)}) %all-to-all-start.1) | async-done | bytes 2097184 | tf_op jit(solution)/shard_map/all_to_all | solution.py:38
  344.9 0.3 convert_reduce_fusion
  345.2 0.2 multiply_reduce_fusion
  345.5 0.7 convolution_convert_fusion.1
  346.2 0.3 concatenate.10
  346.5 0.5 pad_maximum_fusion
  347.1 23.8 %all_to_all.32 = bf16[32,2,4097]{2,1,0:T(2,128)(2,1)S(1)} all-to-all(bf16[32,2,4097]{2,1,0:T(2,128)(2,1)S(1)} %pad_maximum_fusion), channel_id=1, replica_groups=mesh['list'=32,'shard'=16] {'list'}, dimensions={0} | all-to-all | bytes 1048832 | tf_op jit(solution)/shard_map/all_to_all | solution.py:38
  370.9 0.4 reduce.1
  371.4 0.1 slice_reduce_fusion
  371.5 0.6 broadcast_in_dim.8
  372.1 5.5 %all-to-all-start.5 = ((bf16[16,1,2]{2,1,0:T(2,128)(2,1)}), bf16[16,1,2]{2,1,0:T(2,128)(2,1)S(1)}, u32[]{:S(2)}, u32[]{:S(2)}) async-start(bf16[16,1,2]{2,1,0:T(2,128)(2,1)} %broadcast_in_dim.8), calls=%async_computation.5 | async-start | bytes 16384 | tf_op jit(solution)/shard_map/all_to_all | solution.py:15
  377.6 7.3 %all-to-all-done.5 = bf16[16,1,2]{2,1,0:T(2,128)(2,1)S(1)} async-done(((bf16[16,1,2]{2,1,0:T(2,128)(2,1)}), bf16[16,1,2]{2,1,0:T(2,128)(2,1)S(1)}, u32[]{:S(2)}, u32[]{:S(2)}) %all-to-all-start.5) | async-done | bytes 96 | tf_op jit(solution)/shard_map/all_to_all | solution.py:15
  384.9 0.9 broadcast_in_dim.7
  385.8 3.5 all-to-all-start.4
  389.4 0.1 convert_reduce_fusion.2
  389.5 8.6 %all-to-all-done.4 = bf16[16,2,4096]{2,1,0:T(2,128)(2,1)S(1)} async-done(((bf16[16,2,4096]{2,1,0:T(2,128)(2,1)}), bf16[16,2,4096]{2,1,0:T(2,128)(2,1)S(1)}, u32[]{:S(2)}, u32[]{:S(2)}) %all-to-all-start.4) | async-done | bytes 262176 | tf_op jit(solution)/shard_map/all_to_all | solution.py:15
  398.1 0.2 convert_reduce_fusion.1
  398.4 0.7 add_divide_fusion
  399.1 0.5 stack.2
  399.5 24.0 %all_to_all.33 = bf16[32,2,4096]{2,1,0:T(2,128)(2,1)S(1)} all-to-all(bf16[32,2,4096]{2,1,0:T(2,128)(2,1)S(1)} %stack.2), channel_id=1, replica_groups=mesh['list'=32,'shard'=16] {'list'}, dimensions={0} | all-to-all | bytes 1048576 | tf_op jit(solution)/shard_map/all_to_all | solution.py:73
  423.6 0.2 reshape.55
  423.8 0.9 fusion.2
  (20 shorter events, 0.4 us)
Async XLA Ops:
  7.2 179.7 %all-gather.3.cloned.1.call-start = ((), (), s32[]{:S(2)}) async-start(), calls=%async_computation.6 | async-start | bytes 5988352 | tf_op jit(solution)/shard_map/all_gather | solution.py:24
  9.0 257.9 %all-gather.5.cloned.1.call-start = ((), (), s32[]{:S(2)}) async-start(), calls=%async_computation.7 | async-start | bytes 2994176 | tf_op jit(solution)/shard_map/all_gather | solution.py:65
  274.6 19.3 %copy-start.4 = (s32[8]{0:T(128)S(1)}, s32[8]{0:T(128)}, u32[]{:S(2)}) copy-start(s32[8]{0:T(128)} %param.15) | copy-start | bytes 100
  274.6 19.4 %copy-start.3 = (s32[8]{0:T(128)S(1)}, s32[8]{0:T(128)}, u32[]{:S(2)}) copy-start(s32[8]{0:T(128)} %param.14) | copy-start | bytes 100
  274.6 70.6 %copy-start = (bf16[8,4096]{1,0:T(8,128)(2,1)S(1)}, bf16[8,4096]{1,0:T(8,128)(2,1)}, u32[]{:S(2)}) copy-start(bf16[8,4096]{1,0:T(8,128)(2,1)} %param.8) | copy-start | bytes 196612
  274.6 70.8 %copy-start.2 = (f32[4096]{0:T(1024)S(1)}, f32[4096]{0:T(1024)}, u32[]{:S(2)}) copy-start(f32[4096]{0:T(1024)} %param.9) | copy-start | bytes 49156
  274.6 70.3 %all-to-all-start.1 = ((bf16[32,8,4096]{2,1,0:T(8,128)(2,1)}), bf16[32,8,4096]{2,1,0:T(8,128)(2,1)S(1)}, u32[]{:S(2)}, u32[]{:S(2)}) async-start(bf16[32,8,4096]{2,1,0:T(8,128)(2,1)} %fusion), calls=%async_computation.1 | async-start | bytes 4194304 | tf_op jit(solution)/shard_map/all_to_all | solution.py:38
  345.5 52.9 %copy-start.1 = (f32[2,4096]{1,0:T(2,128)S(1)}, f32[2,4096]{1,0:T(2,128)}, u32[]{:S(2)}) copy-start(f32[2,4096]{1,0:T(2,128)} %param.13) | copy-start | bytes 98308
  372.1 12.8 %all-to-all-start.5 = ((bf16[16,1,2]{2,1,0:T(2,128)(2,1)}), bf16[16,1,2]{2,1,0:T(2,128)(2,1)S(1)}, u32[]{:S(2)}, u32[]{:S(2)}) async-start(bf16[16,1,2]{2,1,0:T(2,128)(2,1)} %broadcast_in_dim.8), calls=%async_computation.5 | async-start | bytes 16384 | tf_op jit(solution)/shard_map/all_to_all | solution.py:15
  385.8 12.4 %all-to-all-start.4 = ((bf16[16,2,4096]{2,1,0:T(2,128)(2,1)}), bf16[16,2,4096]{2,1,0:T(2,128)(2,1)S(1)}, u32[]{:S(2)}, u32[]{:S(2)}) async-start(bf16[16,2,4096]{2,1,0:T(2,128)(2,1)} %broadcast_in_dim.7), calls=%async_computation.4 | async-start | bytes 524288 | tf_op jit(solution)/shard_map/all_to_all | solution.py:15
Sparse Core Ops, SparseCore 0:
  10.0 176.8 all-gather.2
  188.9 77.9 all-gather.4
